TPU v7x, 32 devices: a whole 2x2x4 slice. The times are simulated.
32 devices in a mesh: frames: 2 (over core), pix: 16 (over z, y, x).
Axes of the slice: x: 2, y: 2, z: 4, core: 2. Of those that a mesh axis runs over, the one named last changes fastest.
Arguments:
- frames: float32 [256, 32768], P('frames', 'pix'), may hold values from -6 to 6
Outputs:
- sketch: float32 [128, 32768], P(None, 'pix')
- projected: float32 [256, 32768], P('frames', 'pix')
All inputs are finite; a program needn't handle non-finite values.
Results may differ from a plain program's by a relative error of at most 0.0003.
Values sent between devices are 32-bit elements; how exact they have to be, the bound alone decides.
No kernel may reach another device: no remote copies, remote signals or barrier semaphores. Data moves between devices by JAX's collectives and lax.ppermute only.
A program may use at most 64 MiB of HBM per device.

v0:
```python
import jax
import jax.numpy as jnp
from jax import lax
from jax.sharding import PartitionSpec as P


def partner(block, axis, bit):
    count = lax.axis_size(axis)
    route = []
    for low in range(count):
        high = low | 1 << bit
        if high != low and high < count:
            route += [(low, high), (high, low)]
    return lax.ppermute(block, axis, route)


def hdot(left, right):
    return jnp.dot(left, right, precision=lax.Precision.HIGHEST, preferred_element_type=jnp.float32)


def lower_solve(factor, rhs):
    return lax.linalg.triangular_solve(factor, rhs, left_side=True, lower=True)


def rotation(stacked_gram):
    kept = stacked_gram.shape[0] // 2
    subspace = jnp.eye(2 * kept, kept, dtype=jnp.float32)
    product = hdot(stacked_gram, subspace)
    factor = jnp.linalg.cholesky(hdot(product.T, product))
    subspace = lower_solve(factor, product.T).T
    reduced = hdot(subspace.T, hdot(stacked_gram, subspace))
    root_factor = jnp.linalg.cholesky(reduced)
    delta = jnp.trace(reduced) / kept
    damped = jnp.linalg.cholesky(reduced + delta * jnp.eye(kept, dtype=jnp.float32))
    shrunk = lower_solve(damped, reduced)
    whitened = lower_solve(root_factor, subspace.T)
    mixing = hdot(shrunk.T, whitened)
    return (mixing, hdot(shrunk.T, shrunk))


def merge_pair(lower_rows, lower_gram, upper_rows, upper_gram):
    kept = lower_rows.shape[0]
    cross = lax.psum(hdot(lower_rows, upper_rows.T), "pix")
    stacked_gram = jnp.concatenate(
        [
            jnp.concatenate([lower_gram, cross], axis=1),
            jnp.concatenate([cross.T, upper_gram], axis=1),
        ],
        axis=0,
    )
    mixing, new_gram = rotation(stacked_gram)
    merged = hdot(mixing[:, :kept], lower_rows) + hdot(mixing[:, kept:], upper_rows)
    return (merged, new_gram)


def local(frames):
    kept = frames.shape[0]
    sketch = frames
    sketch_gram = lax.psum(hdot(frames, frames.T), "pix")
    position = lax.axis_index("frames")
    span = 1 << 0
    other_rows, other_gram = partner((sketch, sketch_gram), "frames", 0)
    is_upper = position // span % 2 == 1
    lower_rows = jnp.where(is_upper, other_rows, sketch)
    upper_rows = jnp.where(is_upper, sketch, other_rows)
    lower_gram = jnp.where(is_upper, other_gram, sketch_gram)
    upper_gram = jnp.where(is_upper, sketch_gram, other_gram)
    sketch, sketch_gram = merge_pair(lower_rows, lower_gram, upper_rows, upper_gram)
    coeffs = lax.psum(hdot(frames, sketch.T), "pix")
    scaling = 4.0 * kept / (jnp.trace(sketch_gram) + 1e-06)
    projected = hdot(coeffs, sketch) * scaling
    return (sketch, projected)


def solution(mesh):
    return jax.shard_map(
        local,
        mesh=mesh,
        in_specs=(P("frames", "pix"),),
        out_specs=(P(None, "pix"), P("frames", "pix")),
        check_vma=False,
    )
```

profile of v0, /device:TPU:0, one launch (start us, length us, event | category | flops | bytes accessed | tf_op | source)
XLA Modules:
  0.0 313.8 jit_solution(5493166250150651193)
XLA Ops:
  7.2 0.6 collective-permute-start.1
  7.8 3.3 %fusion.28 = f32[128,128]{1,0:T(8,128)} fusion(f32[128,2048]{1,0:T(8,128)} %param.4), kind=kOutput, calls=%fused_computation.51 | convolution fusion | flops 402653184 | bytes 1114112 | tf_op jit(solution)/shard_map/dot_general | solution.py:18
  11.0 1.7 fusion.1
  12.8 109.9 %all-reduce.6.cloned.1.call-done = (f32[128,128]{1,0:T(8,128)}, f32[128,128]{1,0:T(8,128)}) async-done(((f32[128,128]{1,0:T(8,128)}, f32[128,128]{1,0:T(8,128)}), (f32[128,128]{1,0:T(8,128)}, f32[128,128]{1,0:T(8,128)})) %all-reduce.6.cloned.1.call-update) | async-done | bytes 131088 | tf_op jit(solution)/shard_map/psum | solution.py:59
  122.7 1.0 copy.3
  123.7 0.5 collective-permute-done
  124.2 0.3 copy-done.2
  124.8 0.4 fusion.29
  125.3 11.7 %cholesky.59 = f32[128,128]{1,0:T(8,128)S(1)} custom-call(f32[128,128]{1,0:T(8,128)S(1)} %fusion.19), custom_call_target="Cholesky" | custom-call | tf_op jit(solution)/shard_map/jit(cholesky)/cholesky | solution.py:29
  137.1 0.6 compare_reduce_fusion.2
  137.7 0.7 fusion.7
  138.4 9.8 %custom-call.10 = f32[1,128,128]{1,2,0:T(8,128)S(1)} custom-call(f32[1,128,128]{2,1,0:T(8,128)S(1)} %fusion.7), custom_call_target="InvertDiagBlocksLowerTriangular" | custom-call | tf_op jit(solution)/shard_map/triangular_solve/custom-call.0 | solution.py:22
  148.2 0.3 fusion.5
  148.5 0.4 fusion.3
  148.9 0.9 fusion.24
  150.5 11.7 %cholesky.81 = f32[128,128]{1,0:T(8,128)S(1)} custom-call(f32[128,128]{1,0:T(8,128)S(1)} %get-tuple-element.8), custom_call_target="Cholesky" | custom-call | tf_op jit(solution)/shard_map/jit(cholesky)/cholesky | solution.py:32
  162.3 0.6 compare_reduce_fusion
  162.9 0.7 fusion.9
  163.6 9.9 %custom-call.11 = f32[1,128,128]{1,2,0:T(8,128)S(1)} custom-call(f32[1,128,128]{2,1,0:T(8,128)S(1)} %fusion.9), custom_call_target="InvertDiagBlocksLowerTriangular" | custom-call | tf_op jit(solution)/shard_map/triangular_solve/custom-call.0 | solution.py:22
  173.5 0.3 fusion.12
  174.1 11.7 %cholesky.70 = f32[128,128]{1,0:T(8,128)S(1)} custom-call(f32[128,128]{1,0:T(8,128)S(1)} %copy.6), custom_call_target="Cholesky" | custom-call | tf_op jit(solution)/shard_map/jit(cholesky)/cholesky | solution.py:34
  185.8 0.6 compare_reduce_fusion.1
  186.5 0.7 fusion.8
  187.1 9.8 %custom-call.8 = f32[1,128,128]{1,2,0:T(8,128)S(1)} custom-call(f32[1,128,128]{2,1,0:T(8,128)S(1)} %fusion.8), custom_call_target="InvertDiagBlocksLowerTriangular" | custom-call | tf_op jit(solution)/shard_map/triangular_solve | solution.py:22
  196.9 0.3 fusion.15
  197.2 0.3 fusion.30
  197.6 1.0 fusion.2
  198.6 1.0 convolution_add_fusion
  199.6 1.6 convolution_bitcast_fusion
  201.2 0.9 fusion
  202.8 101.3 %all-reduce.4.cloned.1.call-done = f32[128,128]{0,1:T(8,128)} async-done(((f32[128,128]{0,1:T(8,128)}), f32[128,128]{0,1:T(8,128)}) %all-reduce.4.cloned.1.call-update) | async-done | bytes 65552 | tf_op jit(solution)/shard_map/psum | solution.py:69
  304.1 2.9 convolution_multiply_fusion
  (25 shorter events, 0.9 us)
Async XLA Ops:
  7.2 115.6 %all-reduce.6.cloned.1.call-start = ((), (), s32[]{:S(2)}) async-start(), calls=%async_computation.1 | async-start | bytes 262144 | tf_op jit(solution)/shard_map/psum | solution.py:59
  7.2 3.8 %collective-permute-start.1 = (f32[128,2048]{1,0:T(8,128)}, f32[128,2048]{1,0:T(8,128)S(1)}, u32[]{:S(2)}, u32[]{:S(2)}) collective-permute-start(f32[128,2048]{1,0:T(8,128)} %param.4), channel_id=1, source_target_pairs={{0,16},{16,0},{1,17},{17,1},{2,18},{18,2},{3,19},{19,3},{4,20},{20... | collective-permute-start | bytes 3145736 | tf_op jit(solution)/shard_map/ppermute | solution.py:14
  7.8 3.3 %copy-start = (f32[128,2048]{1,0:T(8,128)S(1)}, f32[128,2048]{1,0:T(8,128)}, u32[]{:S(2)}) copy-start(f32[128,2048]{1,0:T(8,128)} %param.4) | copy-start | bytes 3145732
  12.8 291.3 %all-reduce.4.cloned.1.call-start = ((), (), s32[]{:S(2)}) async-start(), calls=%async_computation | async-start | bytes 131072 | tf_op jit(solution)/shard_map/psum | solution.py:69
  122.7 1.5 collective-permute-start
  122.7 1.5 copy-start.3
  123.7 0.8 copy-start.2
  199.6 104.5 %copy-start.1 = (f32[128,2048]{1,0:T(8,128)}, f32[128,2048]{1,0:T(8,128)S(1)}, u32[]{:S(2)}) copy-start(f32[128,2048]{1,0:T(8,128)S(1)} %convolution_add_fusion) | copy-start | bytes 3145732
Sparse Core Ops, SparseCore 0:
  14.1 108.6 all-reduce.5
  201.4 102.6 all-reduce.3
where the time goes:
time: 314 us
  waiting for transfers between devices  212 us (68%)
  other arithmetic  68.7 us (22%)
  matrix products  15.5 us (5%)
  between operations  15.5 us (5%)
    psum x1, waiting for transfers between devices, local(): sketch_gram = lax.psum(hdot(frames, frames.T), 'pix')  110 us
    psum x1, waiting for transfers between devices, local(): coeffs = lax.psum(hdot(frames, sketch.T), 'pix')  101 us
    another operation x6, other arithmetic, lower_solve(): return lax.linalg.triangular_solve(factor, rhs, left_side=True, lower=True)  31.5 us
    dot_general x12, matrix products, hdot(): jnp.dot(left, right, precision=lax.Precision.HIGHEST, preferred_element_t...  14.6 us
    another operation x3, other arithmetic, rotation(): jnp.linalg.cholesky(reduced + delta * jnp.eye(kept, dtype=jnp.float32))  12.4 us
    another operation x3, other arithmetic, rotation(): root_factor = jnp.linalg.cholesky(reduced)  12.4 us
    another operation x3, other arithmetic, rotation(): factor = jnp.linalg.cholesky(hdot(product.T, product))  12.4 us
  transfers between devices with their start and end apart: 4, of which 3 were waited for; matrix products, arithmetic and copies ran while one was open for 2% of the time, Pallas kernels for 0%

commit v1 on v0

--- a/solution.py
+++ b/solution.py
@@ -66,7 +66,7 @@
     lower_gram = jnp.where(is_upper, other_gram, sketch_gram)
     upper_gram = jnp.where(is_upper, sketch_gram, other_gram)
     sketch, sketch_gram = merge_pair(lower_rows, lower_gram, upper_rows, upper_gram)
-    coeffs = lax.psum(hdot(frames, sketch.T), "pix")
+    coeffs = jnp.sum(lax.all_gather(hdot(frames, sketch.T), "pix"), axis=0)
     scaling = 4.0 * kept / (jnp.trace(sketch_gram) + 1e-06)
     projected = hdot(coeffs, sketch) * scaling
     return (sketch, projected)

time: 314 us -> 266 us (0.85)
  waiting for transfers between devices: 212 us -> 163 us
    psum x1 -> x0, waiting for transfers between devices: 101 us -> none  [local(): coeffs = lax.psum(hdot(frames, sketch.T), 'pix')]
    all_gather x0 -> x1, waiting for transfers between devices: none -> 52.6 us  [local(): coeffs = jnp.sum(lax.all_gather(hdot(frames, sketch.T), 'pix'), axis=0)]
where the time goes in v1:
time: 266 us
  waiting for transfers between devices  163 us (61%)
  other arithmetic  68.9 us (26%)
  between operations  15.7 us (6%)
  matrix products  15 us (6%)
  local copies, waits for them, and re-layouts  3.07 us (1%)
    psum x1, waiting for transfers between devices, local(): sketch_gram = lax.psum(hdot(frames, frames.T), 'pix')  110 us
    all_gather x1, waiting for transfers between devices, local(): coeffs = jnp.sum(lax.all_gather(hdot(frames, sketch.T), 'pix'), axis=0)  52.6 us
    another operation x6, other arithmetic, lower_solve(): return lax.linalg.triangular_solve(factor, rhs, left_side=True, lower=True)  31.5 us
    dot_general x12, matrix products, hdot(): jnp.dot(left, right, precision=lax.Precision.HIGHEST, preferred_element_t...  14.1 us
    another operation x3, other arithmetic, rotation(): jnp.linalg.cholesky(reduced + delta * jnp.eye(kept, dtype=jnp.float32))  12.4 us
    another operation x3, other arithmetic, rotation(): root_factor = jnp.linalg.cholesky(reduced)  12.4 us
    another operation x3, other arithmetic, rotation(): factor = jnp.linalg.cholesky(hdot(product.T, product))  12.4 us
  transfers between devices with their start and end apart: 4, of which 3 were waited for; matrix products, arithmetic and copies ran while one was open for 2% of the time, Pallas kernels for 0%

profile of v1, /device:TPU:0, one launch (start us, length us, event | category | flops | bytes accessed | tf_op | source)
XLA Modules:
  0.0 266.1 jit_solution(17558048553783118469)
XLA Ops:
  7.2 0.6 collective-permute-start.1
  7.8 3.5 %fusion.28 = f32[128,128]{1,0:T(8,128)} fusion(f32[128,2048]{1,0:T(8,128)} %param.4), kind=kOutput, calls=%fused_computation.52 | convolution fusion | flops 402653184 | bytes 1114112 | tf_op jit(solution)/shard_map/dot_general | solution.py:18
  11.3 1.7 fusion.1
  13.1 109.7 %all-reduce.3.cloned.1.call-done = (f32[128,128]{1,0:T(8,128)}, f32[128,128]{1,0:T(8,128)}) async-done(((f32[128,128]{1,0:T(8,128)}, f32[128,128]{1,0:T(8,128)}), (f32[128,128]{1,0:T(8,128)}, f32[128,128]{1,0:T(8,128)})) %all-reduce.3.cloned.1.call-update) | async-done | bytes 131088 | tf_op jit(solution)/shard_map/psum | solution.py:59
  122.7 1.0 copy.8
  123.7 0.5 collective-permute-done
  124.2 0.3 copy-done.2
  124.8 0.4 fusion.29
  125.3 11.7 %cholesky.59 = f32[128,128]{1,0:T(8,128)S(1)} custom-call(f32[128,128]{1,0:T(8,128)S(1)} %fusion.19), custom_call_target="Cholesky" | custom-call | tf_op jit(solution)/shard_map/jit(cholesky)/cholesky | solution.py:29
  137.1 0.6 compare_reduce_fusion.2
  137.7 0.7 fusion.7
  138.4 9.8 %custom-call.10 = f32[1,128,128]{1,2,0:T(8,128)S(1)} custom-call(f32[1,128,128]{2,1,0:T(8,128)S(1)} %fusion.7), custom_call_target="InvertDiagBlocksLowerTriangular" | custom-call | tf_op jit(solution)/shard_map/triangular_solve/custom-call.0 | solution.py:22
  148.2 0.3 fusion.5
  148.5 0.4 fusion.3
  148.9 0.9 fusion.24
  150.5 11.7 %cholesky.81 = f32[128,128]{1,0:T(8,128)S(1)} custom-call(f32[128,128]{1,0:T(8,128)S(1)} %get-tuple-element.8), custom_call_target="Cholesky" | custom-call | tf_op jit(solution)/shard_map/jit(cholesky)/cholesky | solution.py:32
  162.3 0.6 compare_reduce_fusion
  162.9 0.7 fusion.9
  163.6 9.9 %custom-call.11 = f32[1,128,128]{1,2,0:T(8,128)S(1)} custom-call(f32[1,128,128]{2,1,0:T(8,128)S(1)} %fusion.9), custom_call_target="InvertDiagBlocksLowerTriangular" | custom-call | tf_op jit(solution)/shard_map/triangular_solve/custom-call.0 | solution.py:22
  173.5 0.3 fusion.12
  174.1 11.7 %cholesky.70 = f32[128,128]{1,0:T(8,128)S(1)} custom-call(f32[128,128]{1,0:T(8,128)S(1)} %copy.11), custom_call_target="Cholesky" | custom-call | tf_op jit(solution)/shard_map/jit(cholesky)/cholesky | solution.py:34
  185.8 0.6 compare_reduce_fusion.1
  186.5 0.7 fusion.8
  187.1 9.8 %custom-call.8 = f32[1,128,128]{1,2,0:T(8,128)S(1)} custom-call(f32[1,128,128]{2,1,0:T(8,128)S(1)} %fusion.8), custom_call_target="InvertDiagBlocksLowerTriangular" | custom-call | tf_op jit(solution)/shard_map/triangular_solve | solution.py:22
  197.2 0.3 fusion.30
  197.6 1.0 fusion.2
  198.6 1.0 convolution_add_fusion
  199.6 1.6 convolution_bitcast_fusion
  201.3 1.0 fusion
  203.0 52.6 %all-gather.3.cloned.1.call-done = f32[2048,128]{0,1:T(8,128)} async-done(((f32[128,128]{0,1:T(8,128)}), f32[2048,128]{0,1:T(8,128)}) %all-gather.3.cloned.1.call-update) | async-done | bytes 1048592 | tf_op jit(solution)/shard_map/all_gather | solution.py:69
  255.6 1.4 copy.13
  257.2 2.0 convolution_multiply_fusion
  (27 shorter events, 1.3 us)
Async XLA Ops:
  7.2 115.6 %all-reduce.3.cloned.1.call-start = ((), (), s32[]{:S(2)}) async-start(), calls=%async_computation.1 | async-start | bytes 262144 | tf_op jit(solution)/shard_map/psum | solution.py:59
  7.2 4.1 %collective-permute-start.1 = (f32[128,2048]{1,0:T(8,128)}, f32[128,2048]{1,0:T(8,128)S(1)}, u32[]{:S(2)}, u32[]{:S(2)}) collective-permute-start(f32[128,2048]{1,0:T(8,128)} %param.4), channel_id=1, source_target_pairs={{0,16},{16,0},{1,17},{17,1},{2,18},{18,2},{3,19},{19,3},{4,20},{20... | collective-permute-start | bytes 3145736 | tf_op jit(solution)/shard_map/ppermute | solution.py:14
  7.8 3.5 %copy-start = (f32[128,2048]{1,0:T(8,128)S(1)}, f32[128,2048]{1,0:T(8,128)}, u32[]{:S(2)}) copy-start(f32[128,2048]{1,0:T(8,128)} %param.4) | copy-start | bytes 3145732
  13.0 242.6 %all-gather.3.cloned.1.call-start = ((), (), s32[]{:S(2)}) async-start(), calls=%async_computation | async-start | bytes 1114112 | tf_op jit(solution)/shard_map/all_gather | solution.py:69
  122.7 1.5 collective-permute-start
  122.7 1.5 copy-start.3
  123.7 0.8 copy-start.2
  199.6 57.6 %copy-start.1 = (f32[128,2048]{1,0:T(8,128)}, f32[128,2048]{1,0:T(8,128)S(1)}, u32[]{:S(2)}) copy-start(f32[128,2048]{1,0:T(8,128)S(1)} %convolution_add_fusion) | copy-start | bytes 3145732
Sparse Core Ops, SparseCore 0:
  14.1 108.6 all-reduce.2
  201.4 54.1 all-gather.2
